TPU v7x, 128 devices: a whole 4x4x4 slice. The times are simulated.
128 devices in a mesh: mem: 4 (over z), lat: 32 (over y, x, core).
Axes of the slice: x: 4, y: 4, z: 4, core: 2. Of those that a mesh axis runs over, the one named last changes fastest.
Arguments:
- ensemble: bfloat16 [32, 72, 32, 1440], P('mem', None, 'lat'), may hold values from -6 to 6
- truth: bfloat16 [72, 32, 1440], P(None, 'lat'), may hold values from -6 to 6
- row_weight: float32 [32], P('lat'), may hold values from 0.3 to 7, as said below
Outputs:
- loss: float32 [], replicated
- gradient: bfloat16 [32, 72, 32, 1440], P('mem', None, 'lat')
Inputs may be any that keep to these rules, and one draw needn't show every extreme that they name: `row_weight`: positive.
All inputs are finite; a program needn't handle non-finite values.
Results may differ from a plain program's by a relative error of at most 0.003.
Values may be sent and summed in bfloat16 or wider, within the bound.
A program may use at most 128 MiB of HBM per device.

v0:
```python
import functools
import jax
import jax.numpy as jnp
from jax import lax
from jax.sharding import Mesh
from jax.sharding import PartitionSpec as P

MEM_LAT = ("mem", "lat_0", "lat_1", "lat_2")
LAT = ("lat_0", "lat_1", "lat_2")


def one_axis_at_a_time(array, axes):
    return functools.reduce(lax.psum, axes, array)


def pair_terms(left, right):
    count_left = left.shape[0]
    grouped = left.reshape((count_left // 2, 2) + left.shape[1:])

    def one_group(block):
        diff = block[:, None] - right[None]
        return (jnp.sum(jnp.abs(diff), axis=1), jnp.sum(jnp.sign(diff), axis=1))

    spread, count = lax.map(one_group, grouped)
    return (spread.reshape(left.shape), count.reshape(left.shape))


def finish(values, target, weight, spread, count, members):
    skill = values - target
    cell = jnp.sum(jnp.abs(skill), axis=0) / members - jnp.sum(spread, axis=0) / (
        2.0 * members * (members - 1)
    )
    partial_value = jnp.sum(weight[None, :, None] * cell)
    grad = (weight[None, None, :, None] * (jnp.sign(skill) - count / (members - 1))).astype(
        jnp.bfloat16
    )
    return (partial_value, grad)


def on_device(ensemble, truth, row_weight):
    local_members, channels, rows, cells = ensemble.shape
    groups = lax.axis_size("mem")
    members = local_members * groups
    values = ensemble.astype(jnp.float32)
    spread, count = pair_terms(
        values, lax.all_gather(ensemble, "mem", axis=0, tiled=True).astype(jnp.float32)
    )
    spread, count = (spread, count)
    partial_value, gradient = finish(
        values, truth.astype(jnp.float32)[None], row_weight, spread, count, members
    )
    total = one_axis_at_a_time(partial_value, MEM_LAT)
    loss = total / (channels * rows * lax.axis_size(LAT) * cells)
    return (loss, gradient)


def solution(mesh):
    torus = Mesh(
        mesh.devices.reshape(mesh.shape["mem"], 4, 4, 2), ("mem", "lat_0", "lat_1", "lat_2")
    )
    in_specs = (P("mem", None, LAT, None), P(None, LAT, None), P(LAT))
    out_specs = (P(), P("mem", None, LAT, None))
    return jax.shard_map(
        on_device, mesh=torus, in_specs=in_specs, out_specs=out_specs, check_vma=False
    )
```

profile of v0, /device:TPU:1, one launch (start us, length us, event | category | flops | bytes accessed | tf_op | source)
XLA Modules:
  0.0 206.8 jit_solution(10314588864462379055)
XLA Ops:
  7.2 0.7 all-gather.2.cloned.1.call-update
  7.9 1.9 convert.5
  10.5 1.7 bitcast_convert_fusion.1
  12.3 72.8 %all-gather.2.cloned.1.call-done = bf16[32,72,1,1440]{3,1,2,0:T(8,128)(2,1)} async-done(((bf16[8,72,1,1440]{3,1,2,0:T(8,128)(2,1)}), bf16[32,72,1,1440]{3,1,2,0:T(8,128)(2,1)}) %all-gather.2.cloned.1.call-update) | async-done | bytes 6635536 | tf_op jit(solution)/shard_map/all_gather | solution.py:46
  85.1 10.1 %bitcast_convert_fusion = f32[32,72,1,1440]{3,1,0,2:T(8,128)} fusion(bf16[32,72,1,1440]{3,1,2,0:T(8,128)(2,1)} %all-gather.2.cloned.1.call-done), kind=kLoop, calls=%fused_computation.7 | loop fusion | flops 3317760 | bytes 19906560 | tf_op jit(solution)/shard_map/while | solution.py:24
  95.2 55.2 %while.12 = (s32[]{:T(128)}, f32[4,2,72,1,1440]{4,2,1,3,0:T(8,128)}, f32[4,2,72,1,1440]{4,2,1,3,0:T(8,128)}, f32[4,2,72,1,1440]{4,2,1,3,0:T(8,128)S(1)}, f32[32,72,1,1440]{3,1,0,2:T(8,128)}, /*index=5*/s32[]{:T(128)}) while((s32[]{:T(128)}, f32[4,2,72,1,1440]{4,2,1,3,0:T(8,128)}, f32[4,2,72,1,1440]{4,2,1,3,0:T(8,128)}, ...), condition=%wide.region_4.5_spmd, body=%wide.region_1.4_spmd.sunk | while | flops 32762880 | bytes 20847176 | solution.py:24
  95.2 12.4 %fusion.3 = (f32[2,72,1440]{2,1,0:T(8,128)S(1)}, f32[2,72,1440]{2,1,0:T(8,128)S(1)}) fusion(f32[32,72,1440]{2,1,0:T(8,128)} %bitcast.27, f32[2,72,1440]{2,1,0:T(8,128)S(1)} %dynamic-slice_bitcast_fusion.2), kind=kLoop, calls=%fused_computation.3.clone.1 | loop fusion | flops 32762880 | bytes 15759360 | tf_op jit(solution)/shard_map/while/body/eval_jaxpr/reduce_sum | solution.py:22
  107.6 1.5 bitcast_dynamic-update-slice_fusion.3
  109.1 12.4 %fusion.3 = (f32[2,72,1440]{2,1,0:T(8,128)S(1)}, f32[2,72,1440]{2,1,0:T(8,128)S(1)}) fusion(f32[32,72,1440]{2,1,0:T(8,128)} %bitcast.27, f32[2,72,1440]{2,1,0:T(8,128)S(1)} %dynamic-slice_bitcast_fusion.2), kind=kLoop, calls=%fused_computation.3.clone.1 | loop fusion | flops 32762880 | bytes 15759360 | tf_op jit(solution)/shard_map/while/body/eval_jaxpr/reduce_sum | solution.py:22
  121.5 1.4 bitcast_dynamic-update-slice_fusion.3
  122.9 12.4 %fusion.3 = (f32[2,72,1440]{2,1,0:T(8,128)S(1)}, f32[2,72,1440]{2,1,0:T(8,128)S(1)}) fusion(f32[32,72,1440]{2,1,0:T(8,128)} %bitcast.27, f32[2,72,1440]{2,1,0:T(8,128)S(1)} %dynamic-slice_bitcast_fusion.2), kind=kLoop, calls=%fused_computation.3.clone.1 | loop fusion | flops 32762880 | bytes 15759360 | tf_op jit(solution)/shard_map/while/body/eval_jaxpr/reduce_sum | solution.py:22
  135.3 1.3 bitcast_dynamic-update-slice_fusion.3
  136.7 12.4 %fusion.3 = (f32[2,72,1440]{2,1,0:T(8,128)S(1)}, f32[2,72,1440]{2,1,0:T(8,128)S(1)}) fusion(f32[32,72,1440]{2,1,0:T(8,128)} %bitcast.27, f32[2,72,1440]{2,1,0:T(8,128)S(1)} %dynamic-slice_bitcast_fusion.2), kind=kLoop, calls=%fused_computation.3.clone.1 | loop fusion | flops 32762880 | bytes 15759360 | tf_op jit(solution)/shard_map/while/body/eval_jaxpr/reduce_sum | solution.py:22
  149.1 1.3 bitcast_dynamic-update-slice_fusion.3
  150.4 4.3 %broadcast_multiply_fusion = f32[4,2,72,1,1440]{4,2,1,3,0:T(8,128)} fusion(f32[4,2,72,1,1440]{4,2,1,3,0:T(8,128)} %get-tuple-element.31), kind=kLoop, calls=%fused_computation.10 | loop fusion | flops 829440 | bytes 6635520 | tf_op jit(solution)/shard_map/div | solution.py:34
  154.7 2.4 %reduce_sum.46 = f32[72,1440]{1,0:T(8,128)S(1)} reduce(f32[4,2,72,1,1440]{4,2,1,3,0:T(8,128)} %get-tuple-element.30, f32[]{:T(128)} %constant.15.clone.1), dimensions={0,1,3}, to_apply=%region_5.6 | reduce | flops 725760 | bytes 3732484 | tf_op jit(solution)/shard_map/reduce_sum | solution.py:30
  157.1 0.1 copy-done
  157.2 0.1 copy-done.1
  157.3 4.8 %multiply_convert_fusion = (bf16[8,72,1,1440]{3,1,2,0:T(8,128)(2,1)}, f32[72,1440]{1,0:T(8,128)S(1)}) fusion(f32[8,72,1,1440]{3,1,2,0:T(8,128)} %bitcast.29, f32[]{:T(128)} %bitcast.26, f32[72,1440]{1,0:T(8,128)S(1)} %copy-done.1, bf16[8,72,1,1440]{3,1,2,0:T(8,128)(2,1)S(1)} %copy-done), kind=kLoop, calls=%fused_computation.8 | loop fusion | flops 6531840 | bytes 7464964 | tf_op jit(solution)/shard_map/convert_element_type | solution.py:34
  162.1 0.7 multiply_reduce_fusion
  162.8 7.5 %psum.28 = f32[]{:T(128)} all-reduce(f32[]{:T(128)} %multiply_reduce_fusion), channel_id=1, replica_groups=mesh['mem'=4,'lat_0'=4,'lat_1'=4,'lat_2'=2] {'mem'}, use_global_device_ids=true, to_apply=%region_7.8 | all-reduce | flops 1 | bytes 8 | tf_op jit(solution)/shard_map/psum | solution.py:13
  170.3 9.2 %psum.29 = f32[]{:T(128)} all-reduce(f32[]{:T(128)} %psum.28), channel_id=1, replica_groups=mesh['mem'=4,'lat_0'=4,'lat_1'=4,'lat_2'=2] {'lat_0'}, use_global_device_ids=true, to_apply=%region_8.9 | all-reduce | flops 1 | bytes 8 | tf_op jit(solution)/shard_map/psum | solution.py:13
  179.5 9.0 %psum.30 = f32[]{:T(128)} all-reduce(f32[]{:T(128)} %psum.29), channel_id=1, replica_groups=mesh['mem'=4,'lat_0'=4,'lat_1'=4,'lat_2'=2] {'lat_1'}, use_global_device_ids=true, to_apply=%region_9.10 | all-reduce | flops 1 | bytes 8 | tf_op jit(solution)/shard_map/psum | solution.py:13
  188.5 9.6 %psum.31 = f32[]{:T(128)} all-reduce(f32[]{:T(128)} %psum.30), channel_id=1, replica_groups=mesh['mem'=4,'lat_0'=4,'lat_1'=4,'lat_2'=2] {'lat_2'}, use_global_device_ids=true, to_apply=%region_10.11 | all-reduce | flops 1 | bytes 8 | tf_op jit(solution)/shard_map/psum | solution.py:13
  (9 shorter events, 0.3 us)
Async XLA Ops:
  7.2 77.9 %all-gather.2.cloned.1.call-start = ((), (), s32[]{:S(2)}) async-start(), calls=%async_computation | async-start | bytes 8847360 | tf_op jit(solution)/shard_map/all_gather | solution.py:46
  154.7 2.5 %copy-start = (bf16[8,72,1,1440]{3,1,2,0:T(8,128)(2,1)S(1)}, bf16[8,72,1,1440]{3,1,2,0:T(8,128)(2,1)}, u32[]{:S(2)}) copy-start(bf16[8,72,1,1440]{3,1,2,0:T(8,128)(2,1)} %param.5) | copy-start | bytes 4976644
  154.7 2.6 %copy-start.1 = (f32[72,1440]{1,0:T(8,128)S(1)}, f32[72,1440]{1,0:T(8,128)}, u32[]{:S(2)}) copy-start(f32[72,1440]{1,0:T(8,128)} %bitcast_convert_fusion.1) | copy-start | bytes 1244164
Sparse Core Ops, SparseCore 0:
  9.6 75.4 all-gather.1
where the time goes:
time: 207 us
  other arithmetic  75.4 us (36%)
  waiting for transfers between devices  73.5 us (36%)
  blocking collectives  35.3 us (17%)
  between operations  16.5 us (8%)
  local copies, waits for them, and re-layouts  5.92 us (3%)
    all_gather x1, waiting for transfers between devices, on_device(): lax.all_gather(ensemble, 'mem', axis=0, tiled=True).astype(jnp.float32)  72.8 us
    reduce_sum x4, other arithmetic, one_group(): return (jnp.sum(jnp.abs(diff), axis=1), jnp.sum(jnp.sign(diff), axis=1))  49.4 us
    psum x4, blocking collectives, one_axis_at_a_time(): return functools.reduce(lax.psum, axes, array)  35.3 us
    while x2, other arithmetic, pair_terms(): spread, count = lax.map(one_group, grouped)  12 us
    dynamic_update_slice x4, local copies, waits for them, and re-layouts, pair_terms(): spread, count = lax.map(one_group, grouped)  5.52 us
    convert_element_type x1, other arithmetic, finish(): (weight[None, None, :, None] * (jnp.sign(skill) - count / (members - 1)))...  4.8 us
    div x1, other arithmetic, finish(): count / (members - 1)  4.27 us
  transfers between devices with their start and end apart: 1, of which 1 were waited for; matrix products, arithmetic and copies ran while one was open for 2% of the time, Pallas kernels for 0%

commit v1 on v0

--- a/solution.py
+++ b/solution.py
@@ -7,6 +7,24 @@
 
 MEM_LAT = ("mem", "lat_0", "lat_1", "lat_2")
 LAT = ("lat_0", "lat_1", "lat_2")
+
+
+def ring_gather(shard, axis, dim):
+    ways, here, turn = (lax.axis_size(axis), lax.axis_index(axis), shard.shape[dim])
+    lengths = [n * ways if d == dim else n for d, n in enumerate(shard.shape)]
+    full = lax.dynamic_update_slice_in_dim(
+        jnp.zeros(lengths, shard.dtype), shard, here * turn, axis=dim
+    )
+    going_up = going_down = shard
+    for far in range(1, ways // 2 + 1):
+        going_up = lax.ppermute(going_up, axis, [(d, (d + 1) % ways) for d in range(ways)])
+        full = lax.dynamic_update_slice_in_dim(full, going_up, (here - far) % ways * turn, axis=dim)
+        if 2 * far < ways:
+            going_down = lax.ppermute(going_down, axis, [(d, (d - 1) % ways) for d in range(ways)])
+            full = lax.dynamic_update_slice_in_dim(
+                full, going_down, (here + far) % ways * turn, axis=dim
+            )
+    return full
 
 
 def one_axis_at_a_time(array, axes):
@@ -42,9 +60,7 @@
     groups = lax.axis_size("mem")
     members = local_members * groups
     values = ensemble.astype(jnp.float32)
-    spread, count = pair_terms(
-        values, lax.all_gather(ensemble, "mem", axis=0, tiled=True).astype(jnp.float32)
-    )
+    spread, count = pair_terms(values, ring_gather(ensemble, "mem", 0).astype(jnp.float32))
     spread, count = (spread, count)
     partial_value, gradient = finish(
         values, truth.astype(jnp.float32)[None], row_weight, spread, count, members

time: 207 us -> 197 us (0.952)
  between operations: 16.5 us -> 3.14 us
  starting transfers between devices: 0.04 us -> 4.73 us
  local copies, waits for them, and re-layouts: 5.92 us -> 9.86 us
  other arithmetic: 75.4 us -> 72.4 us
  waiting for transfers between devices: 73.5 us -> 70.5 us
    all_gather x1 -> x0, waiting for transfers between devices: 72.8 us -> none  [on_device(): lax.all_gather(ensemble, 'mem', axis=0, tiled=True).astype(jnp.float32)]
    ppermute x0 -> x3, waiting for transfers between devices: none -> 70.5 us  [the longest x2 70.5 us: ring_gather(): lax.ppermute(going_up, axis, [(d, (d + 1) % ways) for d in range(ways)])]
    while x2 -> x1, other arithmetic: 12 us -> 1.96 us  [pair_terms(): spread, count = lax.map(one_group, grouped)]
    convert_element_type x0 -> x1, other arithmetic: none -> 7.06 us  [on_device(): ring_gather(ensemble, 'mem', 0).astype(jnp.float32)]
    ppermute x0 -> x3, starting transfers between devices: none -> 4.73 us  [the longest x2 2.53 us: ring_gather(): lax.ppermute(going_up, axis, [(d, (d + 1) % ways) for d in range(ways)])]
    dynamic_update_slice x0 -> x4, local copies, waits for them, and re-layouts: none -> 3.7 us  [the longest x2 1.85 us: ring_gather(): lax.dynamic_update_slice_in_dim(full, going_up, (here - far) % ways * tur...]
  transfers between devices with their start and end apart: 1 -> 3, of which waited for: 1 -> 2; matrix products, arithmetic and copies ran while one was open for 2% -> 4% of each run, Pallas kernels for 0% -> 0%
where the time goes in v1:
time: 197 us
  other arithmetic  72.4 us (37%)
  waiting for transfers between devices  70.5 us (36%)
  blocking collectives  35.9 us (18%)
  local copies, waits for them, and re-layouts  9.86 us (5%)
  starting transfers between devices  4.73 us (2%)
  between operations  3.14 us (2%)
    ppermute x2, waiting for transfers between devices, ring_gather(): lax.ppermute(going_up, axis, [(d, (d + 1) % ways) for d in range(ways)])  70.5 us
    reduce_sum x4, other arithmetic, one_group(): return (jnp.sum(jnp.abs(diff), axis=1), jnp.sum(jnp.sign(diff), axis=1))  49.4 us
    psum x4, blocking collectives, one_axis_at_a_time(): return functools.reduce(lax.psum, axes, array)  35.9 us
    convert_element_type x1, other arithmetic, on_device(): ring_gather(ensemble, 'mem', 0).astype(jnp.float32)  7.06 us
    dynamic_update_slice x4, local copies, waits for them, and re-layouts, pair_terms(): spread, count = lax.map(one_group, grouped)  5.3 us
    convert_element_type x1, other arithmetic, finish(): (weight[None, None, :, None] * (jnp.sign(skill) - count / (members - 1)))...  4.8 us
    div x1, other arithmetic, finish(): count / (members - 1)  4.27 us
  transfers between devices with their start and end apart: 3, of which 2 were waited for; matrix products, arithmetic and copies ran while one was open for 4% of the time, Pallas kernels for 0%

profile of v1, /device:TPU:1, one launch (start us, length us, event | category | flops | bytes accessed | tf_op | source)
XLA Modules:
  0.0 196.6 jit_solution(6937165875739289289)
XLA Ops:
  0.6 2.5 %collective-permute-start = (bf16[8,72,1,1440]{3,1,2,0:T(8,128)(2,1)}, bf16[8,72,1,1440]{3,1,2,0:T(8,128)(2,1)}, u32[]{:S(2)}, u32[]{:S(2)}) collective-permute-start(bf16[8,72,1,1440]{3,1,2,0:T(8,128)(2,1)} %param.5), channel_id=1, source_target_pairs={{0,32},{32,64},{64,96},{96,0},{1,33},{33,65},{65,97},{97,1},{2,34}... | collective-permute-start | bytes 4976648 | tf_op jit(solution)/shard_map/ppermute | solution.py:20
  3.2 2.2 %collective-permute-start.1 = (bf16[8,72,1,1440]{3,1,2,0:T(8,128)(2,1)}, bf16[8,72,1,1440]{3,1,2,0:T(8,128)(2,1)}, u32[]{:S(2)}, u32[]{:S(2)}) collective-permute-start(bf16[8,72,1,1440]{3,1,2,0:T(8,128)(2,1)} %param.5), channel_id=1, source_target_pairs={{0,96},{32,0},{64,32},{96,64},{1,97},{33,1},{65,33},{97,65},{2,98}... | collective-permute-start | bytes 4976648 | tf_op jit(solution)/shard_map/ppermute | solution.py:23
  5.4 2.0 convert.3
  8.0 1.7 bitcast_convert_fusion
  9.7 34.2 %collective-permute-done = bf16[8,72,1,1440]{3,1,2,0:T(8,128)(2,1)} collective-permute-done((bf16[8,72,1,1440]{3,1,2,0:T(8,128)(2,1)}, bf16[8,72,1,1440]{3,1,2,0:T(8,128)(2,1)}, u32[]{:S(2)}, u32[]{:S(2)}) %collective-permute-start) | collective-permute-done | bytes 1658912 | tf_op jit(solution)/shard_map/ppermute | solution.py:20
  44.6 1.7 bitcast_dynamic-update-slice_fusion.4
  46.3 1.7 bitcast_dynamic-update-slice_fusion.3
  47.9 36.3 %collective-permute-done.2 = bf16[8,72,1,1440]{3,1,2,0:T(8,128)(2,1)S(1)} collective-permute-done((bf16[8,72,1,1440]{3,1,2,0:T(8,128)(2,1)}, bf16[8,72,1,1440]{3,1,2,0:T(8,128)(2,1)S(1)}, u32[]{:S(2)}, u32[]{:S(2)}) %collective-permute-start.2) | collective-permute-done | bytes 1658912 | tf_op jit(solution)/shard_map/ppermute | solution.py:20
  84.4 7.1 %convert_element_type.11 = f32[32,72,1,1440]{3,1,0,2:T(8,128)} convert(bf16[32,72,1,1440]{3,1,0,2:T(8,128)(2,1)S(1)} %bitcast_dynamic-update-slice_fusion.2) | non-fusion elementwise | flops 3317760 | bytes 19906560 | tf_op jit(solution)/shard_map/convert_element_type | solution.py:63
  91.5 55.0 %while.12 = (s32[]{:T(128)}, f32[4,2,72,1,1440]{4,2,1,3,0:T(8,128)}, f32[4,2,72,1,1440]{4,2,1,3,0:T(8,128)}, f32[4,2,72,1,1440]{4,2,1,3,0:T(8,128)S(1)}, f32[32,72,1,1440]{3,1,0,2:T(8,128)}, /*index=5*/s32[]{:T(128)}) while((s32[]{:T(128)}, f32[4,2,72,1,1440]{4,2,1,3,0:T(8,128)}, f32[4,2,72,1,1440]{4,2,1,3,0:T(8,128)}, ...), condition=%wide.region_4.5_spmd, body=%wide.region_1.0_spmd.sunk | while | flops 32762880 | bytes 20847176 | solution.py:42
  91.6 12.4 %fusion.3 = (f32[2,72,1440]{2,1,0:T(8,128)S(1)}, f32[2,72,1440]{2,1,0:T(8,128)S(1)}) fusion(f32[32,72,1440]{2,1,0:T(8,128)} %bitcast.32, f32[2,72,1440]{2,1,0:T(8,128)S(1)} %dynamic-slice_bitcast_fusion.2), kind=kLoop, calls=%fused_computation.3.clone.1 | loop fusion | flops 32762880 | bytes 15759360 | tf_op jit(solution)/shard_map/while/body/eval_jaxpr/reduce_sum | solution.py:40
  103.9 1.3 bitcast_dynamic-update-slice_fusion.7
  105.3 12.4 %fusion.3 = (f32[2,72,1440]{2,1,0:T(8,128)S(1)}, f32[2,72,1440]{2,1,0:T(8,128)S(1)}) fusion(f32[32,72,1440]{2,1,0:T(8,128)} %bitcast.32, f32[2,72,1440]{2,1,0:T(8,128)S(1)} %dynamic-slice_bitcast_fusion.2), kind=kLoop, calls=%fused_computation.3.clone.1 | loop fusion | flops 32762880 | bytes 15759360 | tf_op jit(solution)/shard_map/while/body/eval_jaxpr/reduce_sum | solution.py:40
  119.1 12.4 %fusion.3 = (f32[2,72,1440]{2,1,0:T(8,128)S(1)}, f32[2,72,1440]{2,1,0:T(8,128)S(1)}) fusion(f32[32,72,1440]{2,1,0:T(8,128)} %bitcast.32, f32[2,72,1440]{2,1,0:T(8,128)S(1)} %dynamic-slice_bitcast_fusion.2), kind=kLoop, calls=%fused_computation.3.clone.1 | loop fusion | flops 32762880 | bytes 15759360 | tf_op jit(solution)/shard_map/while/body/eval_jaxpr/reduce_sum | solution.py:40
  131.4 1.3 bitcast_dynamic-update-slice_fusion.7
  132.8 12.4 %fusion.3 = (f32[2,72,1440]{2,1,0:T(8,128)S(1)}, f32[2,72,1440]{2,1,0:T(8,128)S(1)}) fusion(f32[32,72,1440]{2,1,0:T(8,128)} %bitcast.32, f32[2,72,1440]{2,1,0:T(8,128)S(1)} %dynamic-slice_bitcast_fusion.2), kind=kLoop, calls=%fused_computation.3.clone.1 | loop fusion | flops 32762880 | bytes 15759360 | tf_op jit(solution)/shard_map/while/body/eval_jaxpr/reduce_sum | solution.py:40
  145.2 1.3 bitcast_dynamic-update-slice_fusion.7
  146.5 4.3 %broadcast_multiply_fusion = f32[4,2,72,1,1440]{4,2,1,3,0:T(8,128)} fusion(f32[4,2,72,1,1440]{4,2,1,3,0:T(8,128)} %get-tuple-element.31), kind=kLoop, calls=%fused_computation.13 | loop fusion | flops 829440 | bytes 6635520 | tf_op jit(solution)/shard_map/div | solution.py:52
  150.8 2.4 %reduce_sum.46 = f32[72,1440]{1,0:T(8,128)S(1)} reduce(f32[4,2,72,1,1440]{4,2,1,3,0:T(8,128)} %get-tuple-element.30, f32[]{:T(128)} %constant.52.clone.1), dimensions={0,1,3}, to_apply=%region_5.6 | reduce | flops 725760 | bytes 3732484 | tf_op jit(solution)/shard_map/reduce_sum | solution.py:48
  153.4 4.8 %multiply_convert_fusion = (bf16[8,72,1,1440]{3,1,2,0:T(8,128)(2,1)}, f32[72,1440]{1,0:T(8,128)S(1)}) fusion(f32[8,72,1,1440]{3,1,2,0:T(8,128)} %bitcast.34, f32[]{:T(128)} %bitcast.31, f32[72,1440]{1,0:T(8,128)S(1)} %copy-done.2, bf16[8,72,1,1440]{3,1,2,0:T(8,128)(2,1)S(1)} %copy-done.1), kind=kLoop, calls=%fused_computation.7 | loop fusion | flops 6531840 | bytes 7464964 | tf_op jit(solution)/shard_map/convert_element_type | solution.py:52
  158.9 6.6 %psum.28 = f32[]{:T(128)} all-reduce(f32[]{:T(128)} %multiply_reduce_fusion), channel_id=1, replica_groups=mesh['mem'=4,'lat_0'=4,'lat_1'=4,'lat_2'=2] {'mem'}, use_global_device_ids=true, to_apply=%region_7.8 | all-reduce | flops 1 | bytes 8 | tf_op jit(solution)/shard_map/psum | solution.py:31
  165.5 9.3 %psum.29 = f32[]{:T(128)} all-reduce(f32[]{:T(128)} %psum.28), channel_id=1, replica_groups=mesh['mem'=4,'lat_0'=4,'lat_1'=4,'lat_2'=2] {'lat_0'}, use_global_device_ids=true, to_apply=%region_8.9 | all-reduce | flops 1 | bytes 8 | tf_op jit(solution)/shard_map/psum | solution.py:31
  174.9 9.2 %psum.30 = f32[]{:T(128)} all-reduce(f32[]{:T(128)} %psum.29), channel_id=1, replica_groups=mesh['mem'=4,'lat_0'=4,'lat_1'=4,'lat_2'=2] {'lat_1'}, use_global_device_ids=true, to_apply=%region_9.10 | all-reduce | flops 1 | bytes 8 | tf_op jit(solution)/shard_map/psum | solution.py:31
  184.0 10.8 %psum.31 = f32[]{:T(128)} all-reduce(f32[]{:T(128)} %psum.30), channel_id=1, replica_groups=mesh['mem'=4,'lat_0'=4,'lat_1'=4,'lat_2'=2] {'lat_2'}, use_global_device_ids=true, to_apply=%region_10.11 | all-reduce | flops 1 | bytes 8 | tf_op jit(solution)/shard_map/psum | solution.py:31
  (19 shorter events, 3.3 us)
Async XLA Ops:
  0.6 43.3 %collective-permute-start = (bf16[8,72,1,1440]{3,1,2,0:T(8,128)(2,1)}, bf16[8,72,1,1440]{3,1,2,0:T(8,128)(2,1)}, u32[]{:S(2)}, u32[]{:S(2)}) collective-permute-start(bf16[8,72,1,1440]{3,1,2,0:T(8,128)(2,1)} %param.5), channel_id=1, source_target_pairs={{0,32},{32,64},{64,96},{96,0},{1,33},{33,65},{65,97},{97,1},{2,34}... | collective-permute-start | bytes 4976648 | tf_op jit(solution)/shard_map/ppermute | solution.py:20
  3.2 43.1 %collective-permute-start.1 = (bf16[8,72,1,1440]{3,1,2,0:T(8,128)(2,1)}, bf16[8,72,1,1440]{3,1,2,0:T(8,128)(2,1)}, u32[]{:S(2)}, u32[]{:S(2)}) collective-permute-start(bf16[8,72,1,1440]{3,1,2,0:T(8,128)(2,1)} %param.5), channel_id=1, source_target_pairs={{0,96},{32,0},{64,32},{96,64},{1,97},{33,1},{65,33},{97,65},{2,98}... | collective-permute-start | bytes 4976648 | tf_op jit(solution)/shard_map/ppermute | solution.py:23
  9.7 34.6 %copy-start = (bf16[8,72,1,1440]{3,1,2,0:T(8,128)(2,1)S(1)}, bf16[8,72,1,1440]{3,1,2,0:T(8,128)(2,1)}, u32[]{:S(2)}) copy-start(bf16[8,72,1,1440]{3,1,2,0:T(8,128)(2,1)} %param.5) | copy-start | bytes 4976644
  43.9 40.3 %collective-permute-start.2 = (bf16[8,72,1,1440]{3,1,2,0:T(8,128)(2,1)}, bf16[8,72,1,1440]{3,1,2,0:T(8,128)(2,1)S(1)}, u32[]{:S(2)}, u32[]{:S(2)}) collective-permute-start(bf16[8,72,1,1440]{3,1,2,0:T(8,128)(2,1)} %collective-permute-done), channel_id=1, source_target_pairs={{0,32},{32,64},{64,96},{96,0},{1,33},{33,65},{65,97},{97,1},{2,34}... | collective-permute-start | bytes 4976648 | tf_op jit(solution)/shard_map/ppermute | solution.py:20
  150.8 2.5 %copy-start.1 = (bf16[8,72,1,1440]{3,1,2,0:T(8,128)(2,1)S(1)}, bf16[8,72,1,1440]{3,1,2,0:T(8,128)(2,1)}, u32[]{:S(2)}) copy-start(bf16[8,72,1,1440]{3,1,2,0:T(8,128)(2,1)} %param.5) | copy-start | bytes 4976644
  150.8 2.6 %copy-start.2 = (f32[72,1440]{1,0:T(8,128)S(1)}, f32[72,1440]{1,0:T(8,128)}, u32[]{:S(2)}) copy-start(f32[72,1440]{1,0:T(8,128)} %bitcast_convert_fusion) | copy-start | bytes 1244164
